TPU v7x, 512 devices: a 8x2x16 block of a 8x8x16 slice. The times are simulated.
512 devices in a mesh: frag: 2 (over y), band: 128 (over z, x), slab: 2 (over core).
Axes of the slice: x: 8, y: 2, z: 16, core: 2. Of those that a mesh axis runs over, the one named last changes fastest.
The devices are a block of a 8x8x16 slice.
Arguments:
- wavefunctions: bfloat16 [2048, 16384], P('band', ('frag', 'slab')), parts along dimension 1, may hold values from -6 to 6
- eigvec: bfloat16 [2048, 4096], P(None, ('frag', 'band', 'slab')), parts along dimension 1, may hold values from -1 to 1, as said below
- occupation: float32 [4096], P('frag'), parts along dimension 0, may hold values from 0.1 to 2
Outputs:
- rotated: float32 [2048, 16384], P('band', ('frag', 'slab')), parts along dimension 1
- density: float32 [16384], P(('frag', 'slab')), parts along dimension 0
There are 2 independent parts, one for each index of `frag`. A program takes and returns all parts, laid end to end along the dimension named above; each array names one. Nothing has to cross between parts.
Inputs may be any that keep to these rules, and one draw needn't show every extreme that they name: eigvec is an orthogonal matrix rounded to bfloat16.
All inputs are finite; a program needn't handle non-finite values.
Results may differ from a plain program's by a relative error of at most 0.0003.
Values may be sent and summed in bfloat16 or wider, within the bound.
No kernel may reach another device: no remote copies, remote signals or barrier semaphores. Data moves between devices by JAX's collectives and lax.ppermute only.
A program may use at most 64 MiB of HBM per device.

v0:
```python
import jax
import jax.numpy as jnp
from jax import lax
from jax.sharding import Mesh
from jax.sharding import PartitionSpec as P

BAND = ("band_0", "band_1")
BAND_SLAB = ("band_0", "band_1", "slab")
FRAG_BAND_SLAB = ("frag", "band_0", "band_1", "slab")


def in_blocks(array, dim, peers):
    dims = array.shape
    blocks = array.reshape(*dims[:dim], peers, dims[dim] // peers, *dims[dim + 1 :])
    return jnp.moveaxis(blocks, dim, 0)


def laid_out(blocks, dim):
    blocks = jnp.moveaxis(blocks, 0, dim)
    dims = blocks.shape
    return blocks.reshape(*dims[:dim], dims[dim] * dims[dim + 1], *dims[dim + 2 :])


def exchange_in_order(blocks, axes, turns):
    inside = blocks.shape[1:]
    result = blocks.reshape(*(lax.axis_size(a) for a in axes), *inside)
    for k in turns:
        result = lax.all_to_all(result, axes[k], k, k, tiled=True)
    return result.reshape(-1, *inside)


def one_axis_at_a_time(array, axes, turns, split_dim, concat_dim):
    blocks = in_blocks(array, split_dim, lax.axis_size(axes))
    return laid_out(exchange_in_order(blocks, axes, turns), concat_dim)


def stacked_from(array, axes, turns):
    blocks = array
    for k in turns:
        blocks = lax.all_gather(blocks, axes[k])
    done = turns[::-1]
    back = [done.index(k) for k in range(len(axes))]
    blocks = blocks.transpose(*back, *range(len(axes), blocks.ndim))
    return blocks.reshape(-1, *array.shape)


def whole_of(array, axes, turns, dim):
    return laid_out(stacked_from(array, axes, turns), dim)


def local(wavefunctions, eigvec, occupation):
    total_bands = eigvec.shape[0]
    by_points = one_axis_at_a_time(wavefunctions, BAND, (0, 1), 1, 0)
    point_rows = lax.dot_general(
        lax.all_gather(eigvec, BAND_SLAB, axis=1, tiled=True),
        by_points,
        (((0,), (0,)), ((), ())),
        preferred_element_type=jnp.float32,
    )
    rotated = lax.all_to_all(point_rows, BAND, split_axis=0, concat_axis=1, tiled=True)
    local_density = jnp.dot(
        occupation,
        point_rows * point_rows,
        precision=lax.Precision.HIGHEST,
        preferred_element_type=jnp.float32,
    ) / jnp.float32(total_bands)
    density = whole_of(local_density, BAND, (0, 1), 0)
    return (rotated, density)


def solution(mesh):
    torus = Mesh(
        mesh.devices.reshape(mesh.shape["frag"], 16, 8, mesh.shape["slab"]),
        ("frag", "band_0", "band_1", "slab"),
    )
    in_specs = (P(BAND, ("frag", "slab")), P(None, FRAG_BAND_SLAB), P("frag"))
    out_specs = (P(BAND, ("frag", "slab")), P(("frag", "slab")))
    return jax.shard_map(local, mesh=torus, in_specs=in_specs, out_specs=out_specs, check_vma=False)
```

profile of v0, /device:TPU:80, one launch (start us, length us, event | category | flops | bytes accessed | tf_op | source)
XLA Modules:
  0.0 286.6 jit_solution(17181273735163144986)
XLA Ops:
  7.2 0.0 copy-start
  7.2 0.1 all-gather.4.cloned.1.call-start
  7.3 0.7 all-gather.4.cloned.1.call-update
  8.0 1.3 reshape.13
  9.3 0.3 copy.18
  9.6 0.5 reshape.24
  10.2 58.1 %all_to_all.29 = bf16[16,2,2048]{2,1,0:T(2,128)(2,1)S(1)} all-to-all(bf16[16,2,2048]{2,1,0:T(2,128)(2,1)S(1)} %reshape.24), channel_id=1, replica_groups=mesh['frag'=2,'band_0'=16,'band_1'=8,'slab'=2] {'band_0'}, dimensions={0} | all-to-all | bytes 262144 | tf_op jit(solution)/shard_map/all_to_all | solution.py:28
  68.3 0.3 reshape.25
  68.6 0.5 reshape.26
  69.1 16.2 %all_to_all.30 = bf16[8,2,4096]{2,1,0:T(2,128)(2,1)S(1)} all-to-all(bf16[8,2,4096]{2,1,0:T(2,128)(2,1)S(1)} %reshape.26), channel_id=1, replica_groups=mesh['frag'=2,'band_0'=16,'band_1'=8,'slab'=2] {'band_1'}, dimensions={0} | all-to-all | bytes 262144 | tf_op jit(solution)/shard_map/all_to_all | solution.py:28
  85.3 0.3 reshape.27
  85.6 106.7 %all-gather.4.cloned.1.call-done = bf16[2048,2048]{0,1:T(8,128)(2,1)} async-done(((bf16[2048,8]{0,1:T(8,128)(2,1)}), bf16[2048,2048]{0,1:T(8,128)(2,1)}) %all-gather.4.cloned.1.call-update) | async-done | bytes 8388624 | tf_op jit(solution)/shard_map/all_gather | solution.py:55
  192.4 5.9 %fusion.2 = f32[2048,32]{0,1:T(8,128)S(1)} fusion(bf16[2048,2048]{0,1:T(8,128)(2,1)} %all-gather.4.cloned.1.call-done, bf16[2048,32]{1,0:T(8,128)(2,1)S(1)} %bitcast.25), kind=kOutput, calls=%fused_computation.4 | convolution fusion | flops 268435456 | bytes 8781824 | tf_op jit(solution)/shard_map/dot_general | solution.py:54
  198.3 0.3 copy.21
  198.7 1.2 reshape.28
  199.8 16.5 %all-to-all-start.2 = ((f32[128,1,512]{2,1,0:T(1,128)}), f32[128,1,512]{2,1,0:T(1,128)S(1)}, u32[]{:S(2)}, u32[]{:S(2)}) async-start(f32[128,1,512]{2,1,0:T(1,128)} %reshape.28), calls=%async_computation.2 | async-start | bytes 524288 | tf_op jit(solution)/shard_map/all_to_all | solution.py:60
  216.3 1.3 dynamic-slice
  218.2 0.0 copy-done
  218.2 0.3 fusion
  218.5 0.2 dynamic-update-slice
  218.7 30.8 %all-reduce = f32[512]{0:T(512)S(1)} all-reduce(f32[512]{0:T(512)S(1)} %dynamic-update-slice), channel_id=2, replica_groups=mesh['frag'=2,'band_0'=16,'band_1'=8,'slab'=2] {'band_0'}, use_global_device_ids=true, to_apply=%add | all-reduce | flops 512 | bytes 4096
  249.6 0.1 reshape.15
  249.6 25.8 %all-gather.1 = f32[128,32]{1,0:T(8,128)S(1)} all-gather(f32[16,32]{1,0:T(8,128)S(1)} %reshape.15), channel_id=3, replica_groups=mesh['frag'=2,'band_0'=16,'band_1'=8,'slab'=2] {'band_1'}, dimensions={0}, use_global_device_ids=true | all-gather | bytes 18432 | tf_op jit(solution)/shard_map/all_gather | solution.py:40
  275.4 0.7 reshape_reshape.7
  276.1 0.0 all-to-all-done.2
  276.1 0.5 broadcast.2
  276.6 1.3 reduce
  277.9 0.3 reshape.29
  278.2 0.3 copy.22
  278.5 1.2 all_to_all.25
  (4 shorter events, 0.1 us)
Async XLA Ops:
  7.2 211.1 %copy-start = (f32[2048]{0:T(1024)S(1)}, f32[2048]{0:T(1024)}, u32[]{:S(2)}) copy-start(f32[2048]{0:T(1024)} %param.5) | copy-start | bytes 24580
  7.2 185.2 %all-gather.4.cloned.1.call-start = ((), (), s32[]{:S(2)}) async-start(), calls=%async_computation.3 | async-start | bytes 8421376 | tf_op jit(solution)/shard_map/all_gather | solution.py:55
  199.8 76.3 %all-to-all-start.2 = ((f32[128,1,512]{2,1,0:T(1,128)}), f32[128,1,512]{2,1,0:T(1,128)S(1)}, u32[]{:S(2)}, u32[]{:S(2)}) async-start(f32[128,1,512]{2,1,0:T(1,128)} %reshape.28), calls=%async_computation.2 | async-start | bytes 524288 | tf_op jit(solution)/shard_map/all_to_all | solution.py:60
Sparse Core Ops, SparseCore 0:
  11.2 181.1 all-gather.3
where the time goes:
time: 288 us; the launch traced here: 287 us
  blocking collectives  131 us (45%)
  waiting for transfers between devices  107 us (37%)
  starting transfers between devices  16.5 us (6%)
  between operations  14.8 us (5%)
  local copies, waits for them, and re-layouts  9.42 us (3%)
  matrix products  6.21 us (2%)
    all_gather x1, waiting for transfers between devices, local(): lax.all_gather(eigvec, BAND_SLAB, axis=1, tiled=True)  107 us
    all_to_all x2, blocking collectives, exchange_in_order(): result = lax.all_to_all(result, axes[k], k, k, tiled=True)  74.3 us
    unnamed x1, blocking collectives  30.8 us
    all_gather x1, blocking collectives, stacked_from(): blocks = lax.all_gather(blocks, axes[k])  25.8 us
    all_to_all x1, starting transfers between devices, local(): lax.all_to_all(point_rows, BAND, split_axis=0, concat_axis=1, tiled=True)  16.5 us
    dot_general x1, matrix products, local(): lax.dot_general(lax.all_gather(eigvec, BAND_SLAB, axis=1, tiled=True), by...  5.94 us
  transfers between devices with their start and end apart: 2, of which 1 were waited for; matrix products, arithmetic and copies ran while one was open for 2% of the time, Pallas kernels for 0%

commit v1 on v0

v1 whole, which is shorter than its diff:
```python
import jax
import jax.numpy as jnp
from jax import lax
from jax.sharding import Mesh
from jax.sharding import PartitionSpec as P

Z = ("zh", "zl")
BAND = ("zh", "zl", "x")


def gathered(array, axis):
    peers = lax.axis_size(axis)
    copies = jnp.broadcast_to(array[None], (peers, *array.shape))
    return lax.all_to_all(copies, axis, 0, 0, tiled=True)


def local(wavefunctions, eigvec, occupation):
    zs, zh, zl, xs, cores = (lax.axis_size(a) for a in (Z, "zh", "zl", "x", "slab"))
    bands, cols = eigvec.shape
    own = wavefunctions.shape[0]
    points = wavefunctions.shape[1] // zs
    pair = xs // zl
    run = zs * own
    quarters = eigvec.T.reshape(cols, zs, xs, own).transpose(2, 0, 1, 3)
    quarters = quarters.reshape(zl, pair, cols, run).transpose(0, 2, 1, 3)
    quarters = quarters.reshape(1, zl, -1, points)
    quarters = jnp.broadcast_to(quarters, (zh, *quarters.shape[1:])).reshape(zs, -1, points)
    blocks = wavefunctions.reshape(own, zs, points).transpose(1, 0, 2)
    met = lax.all_to_all(jnp.concatenate([blocks, quarters], 1), Z, 0, 0, tiled=True)
    old = gathered(met[:, :own].reshape(run, points), "x").reshape(zl, pair, run, points)
    mine = lax.all_gather(met[:, own:].reshape(zs * cols * pair, run), "zl")
    other = lax.ppermute(mine, "slab", [(k, (k + 1) % cores) for k in range(cores)])
    first = lax.axis_index("slab") == 0
    panels = jnp.stack([jnp.where(first, mine, other), jnp.where(first, other, mine)])
    columns = panels.reshape(cores, zl, zs, cols, pair, run).transpose(2, 0, 3, 1, 4, 5)
    columns = columns.reshape(run, bands)
    new = lax.dot_general(
        columns, old.reshape(bands, points), (((1,), (0,)), ((), ())), preferred_element_type=jnp.float32
    )
    weights = lax.dynamic_index_in_dim(occupation.reshape(zs, xs, own), lax.axis_index("x"), 1, False)
    partial = jnp.sum(weights.reshape(run, 1) * new * new, axis=0)
    density = jnp.sum(gathered(partial[None], "x"), axis=0) / jnp.float32(bands)
    sent = jnp.concatenate(
        [new.reshape(zs, own * points), jnp.broadcast_to(density, (zs, points))], axis=1
    )
    got = lax.all_to_all(sent[:, None], Z, 0, 0, tiled=True).reshape(zs, own + 1, points)
    rotated = got[:, :own].transpose(1, 0, 2).reshape(own, zs * points)
    return rotated, got[:, own].reshape(zs * points)


def solution(mesh):
    torus = Mesh(
        mesh.devices.reshape(mesh.shape["frag"], 4, 4, 8, mesh.shape["slab"]),
        ("frag", "zh", "zl", "x", "slab"),
    )
    in_specs = (P(BAND, ("frag", "slab")), P(None, ("frag", *BAND, "slab")), P("frag"))
    out_specs = (P(BAND, ("frag", "slab")), P(("frag", "slab")))
    return jax.shard_map(local, mesh=torus, in_specs=in_specs, out_specs=out_specs, check_vma=False)
```

time: 288 us -> 140 us (0.49)
  waiting for transfers between devices: 107 us -> 10.8 us
  blocking collectives: 131 us -> 104 us
  between operations: 14.8 us -> 0.82 us
  matrix products: 6.21 us -> 0.45 us
    all_gather x1 -> x0, waiting for transfers between devices: 107 us -> none  [local(): lax.all_gather(eigvec, BAND_SLAB, axis=1, tiled=True)]
    unnamed x1 -> x0, blocking collectives: 30.8 us -> none
    all_to_all x2, blocking collectives: 74.3 us -> 88.5 us  [the longest x1 61.6 us: local(): lax.all_to_all(jnp.concatenate([blocks, quarters], 1), Z, 0, 0, tiled=True)]
    all_gather x1, blocking collectives: 25.8 us -> 15.5 us  [local(): mine = lax.all_gather(met[:, own:].reshape(zs * cols * pair, run), 'zl')]
    all_to_all x1 -> x2, waiting for transfers between devices: 0.01 us -> 9.78 us  [gathered(): return lax.all_to_all(copies, axis, 0, 0, tiled=True)]
    dot_general x2 -> x1, matrix products: 6.21 us -> 0.45 us  [local(): lax.dot_general(columns, old.reshape(bands, points), (((1,), (0,)), ((),...]
    all_to_all x1 -> x2, starting transfers between devices: 16.5 us -> 12.4 us  [gathered(): return lax.all_to_all(copies, axis, 0, 0, tiled=True)]
  transfers between devices with their start and end apart: 2 -> 3, of which waited for: 1 -> 3; matrix products, arithmetic and copies ran while one was open for 2% -> 2% of each run, Pallas kernels for 0% -> 0%
where the time goes in v1:
time: 140 us; the launch traced here: 139 us
  blocking collectives  104 us (74%)
  starting transfers between devices  14.4 us (10%)
  waiting for transfers between devices  10.8 us (8%)
  local copies, waits for them, and re-layouts  7.04 us (5%)
  other arithmetic  2.02 us (1%)
    all_to_all x1, blocking collectives, local(): lax.all_to_all(jnp.concatenate([blocks, quarters], 1), Z, 0, 0, tiled=True)  61.6 us
    all_to_all x1, blocking collectives, local(): lax.all_to_all(sent[:, None], Z, 0, 0, tiled=True)  26.9 us
    all_gather x1, blocking collectives, local(): mine = lax.all_gather(met[:, own:].reshape(zs * cols * pair, run), 'zl')  15.5 us
    all_to_all x2, starting transfers between devices, gathered(): return lax.all_to_all(copies, axis, 0, 0, tiled=True)  12.4 us
    all_to_all x2, waiting for transfers between devices, gathered(): return lax.all_to_all(copies, axis, 0, 0, tiled=True)  9.78 us
  transfers between devices with their start and end apart: 3, of which 3 were waited for; matrix products, arithmetic and copies ran while one was open for 2% of the time, Pallas kernels for 0%

profile of v1, /device:TPU:80, one launch (start us, length us, event | category | flops | bytes accessed | tf_op | source)
XLA Modules:
  0.0 139.5 jit_solution(8607598919132796651)
XLA Ops:
  0.6 0.0 copy-start
  0.6 0.9 copy.38
  1.6 0.0 copy-done
  1.6 0.2 reshape.51
  1.9 0.2 reshape.52
  2.2 0.1 copy.30
  2.3 61.6 %all_to_all.20 = bf16[16,32,256]{2,1,0:T(8,128)(2,1)S(1)} all-to-all(bf16[16,32,256]{2,1,0:T(8,128)(2,1)S(1)} %copy.30), channel_id=1, replica_groups=mesh['frag'=2,'zh'=4,'zl'=4,'x'=8,'slab'=2] {'zh','zl'}, dimensions={0} | all-to-all | bytes 524288 | tf_op jit(solution)/shard_map/all_to_all | solution.py:29
  64.0 1.1 broadcast_in_dim.30
  65.0 7.3 %all-to-all-start.1 = ((bf16[8,256,256]{2,1,0:T(8,128)(2,1)}), bf16[8,256,256]{2,1,0:T(8,128)(2,1)S(1)}, u32[]{:S(2)}, u32[]{:S(2)}) async-start(bf16[8,256,256]{2,1,0:T(8,128)(2,1)} %broadcast_in_dim.30), calls=%async_computation.1 | async-start | bytes 2097152 | tf_op jit(solution)/shard_map/all_to_all | solution.py:14
  72.3 15.5 %all_gather.3 = bf16[4,256,256]{2,1,0:T(8,128)(2,1)S(1)} all-gather(bf16[1,256,256]{2,1,0:T(8,128)(2,1)S(1)} %bitcast.28), channel_id=1, replica_groups=mesh['frag'=2,'zh'=4,'zl'=4,'x'=8,'slab'=2] {'zl'}, dimensions={0}, use_global_device_ids=true | all-gather | bytes 655360 | tf_op jit(solution)/shard_map/all_gather | solution.py:31
  87.9 1.9 %collective-permute-start = (bf16[4,256,256]{2,1,0:T(8,128)(2,1)S(1)}, bf16[4,256,256]{2,1,0:T(8,128)(2,1)S(1)}, u32[]{:S(2)}, u32[]{:S(2)}) collective-permute-start(bf16[4,256,256]{2,1,0:T(8,128)(2,1)S(1)} %all_gather.3), channel_id=1, source_target_pairs={{0,1},{1,0},{2,3},{3,2},{4,5},{5,4},{6,7},{7,6},{8,9},{9,8},{10,11... | collective-permute-start | bytes 1572872 | tf_op jit(solution)/shard_map/ppermute | solution.py:32
  89.8 0.0 copy-start.1
  89.8 0.7 copy-done.1
  90.5 0.1 reshape.56
  90.7 0.1 mul.13
  90.7 1.0 collective-permute-done
  91.7 0.1 broadcast_select_fusion.1
  91.8 0.2 stack.9
  92.0 0.2 stack.10
  92.2 1.2 copy_bitcast_fusion
  93.4 0.8 reshape.54
  94.2 2.1 %all-to-all-done.1 = bf16[8,256,256]{2,1,0:T(8,128)(2,1)S(1)} async-done(((bf16[8,256,256]{2,1,0:T(8,128)(2,1)}), bf16[8,256,256]{2,1,0:T(8,128)(2,1)S(1)}, u32[]{:S(2)}, u32[]{:S(2)}) %all-to-all-start.1) | async-done | bytes 1048608 | tf_op jit(solution)/shard_map/all_to_all | solution.py:14
  96.3 0.5 fusion
  96.8 0.6 broadcast_in_dim.31
  97.4 5.1 %all-to-all-start.2 = ((f32[8,1,256]{2,1,0:T(1,128)}), f32[8,1,256]{2,1,0:T(1,128)S(1)}, u32[]{:S(2)}, u32[]{:S(2)}) async-start(f32[8,1,256]{2,1,0:T(1,128)} %broadcast_in_dim.31), calls=%async_computation.2 | async-start | bytes 16384 | tf_op jit(solution)/shard_map/all_to_all | solution.py:14
  102.5 0.1 reshape.55
  102.6 7.7 %all-to-all-done.2 = f32[8,1,256]{2,1,0:T(1,128)S(1)} async-done(((f32[8,1,256]{2,1,0:T(1,128)}), f32[8,1,256]{2,1,0:T(1,128)S(1)}, u32[]{:S(2)}, u32[]{:S(2)}) %all-to-all-start.2) | async-done | bytes 8224 | tf_op jit(solution)/shard_map/all_to_all | solution.py:14
  110.3 0.2 broadcast_in_dim.33
  110.5 26.9 %all_to_all.21 = f32[16,1,4352]{2,1,0:T(1,128)S(1)} all-to-all(f32[16,1,4352]{2,1,0:T(1,128)S(1)} %broadcast_in_dim.33), channel_id=1, replica_groups=mesh['frag'=2,'zh'=4,'zl'=4,'x'=8,'slab'=2] {'zh','zl'}, dimensions={0} | all-to-all | bytes 557056 | tf_op jit(solution)/shard_map/all_to_all | solution.py:46
  137.4 0.7 reduce.2
  138.1 0.6 slice.19
  138.7 0.7 copy.37
  (13 shorter events, 0.3 us)
Async XLA Ops:
  0.6 0.9 copy-start
  65.0 31.3 %all-to-all-start.1 = ((bf16[8,256,256]{2,1,0:T(8,128)(2,1)}), bf16[8,256,256]{2,1,0:T(8,128)(2,1)S(1)}, u32[]{:S(2)}, u32[]{:S(2)}) async-start(bf16[8,256,256]{2,1,0:T(8,128)(2,1)} %broadcast_in_dim.30), calls=%async_computation.1 | async-start | bytes 2097152 | tf_op jit(solution)/shard_map/all_to_all | solution.py:14
  87.9 3.8 %collective-permute-start = (bf16[4,256,256]{2,1,0:T(8,128)(2,1)S(1)}, bf16[4,256,256]{2,1,0:T(8,128)(2,1)S(1)}, u32[]{:S(2)}, u32[]{:S(2)}) collective-permute-start(bf16[4,256,256]{2,1,0:T(8,128)(2,1)S(1)} %all_gather.3), channel_id=1, source_target_pairs={{0,1},{1,0},{2,3},{3,2},{4,5},{5,4},{6,7},{7,6},{8,9},{9,8},{10,11... | collective-permute-start | bytes 1572872 | tf_op jit(solution)/shard_map/ppermute | solution.py:32
  89.8 0.7 copy-start.1
  97.4 12.8 %all-to-all-start.2 = ((f32[8,1,256]{2,1,0:T(1,128)}), f32[8,1,256]{2,1,0:T(1,128)S(1)}, u32[]{:S(2)}, u32[]{:S(2)}) async-start(f32[8,1,256]{2,1,0:T(1,128)} %broadcast_in_dim.31), calls=%async_computation.2 | async-start | bytes 16384 | tf_op jit(solution)/shard_map/all_to_all | solution.py:14

commit v2 on v1

--- a/solution.py
+++ b/solution.py
@@ -12,6 +12,10 @@
     peers = lax.axis_size(axis)
     copies = jnp.broadcast_to(array[None], (peers, *array.shape))
     return lax.all_to_all(copies, axis, 0, 0, tiled=True)
+
+
+def exponent(largest):
+    return jnp.clip(jnp.floor(jnp.log2(jnp.maximum(largest, 1e-37))), -120.0, 120.0)
 
 
 def local(wavefunctions, eigvec, occupation):
@@ -39,13 +43,25 @@
     )
     weights = lax.dynamic_index_in_dim(occupation.reshape(zs, xs, own), lax.axis_index("x"), 1, False)
     partial = jnp.sum(weights.reshape(run, 1) * new * new, axis=0)
-    density = jnp.sum(gathered(partial[None], "x"), axis=0) / jnp.float32(bands)
-    sent = jnp.concatenate(
-        [new.reshape(zs, own * points), jnp.broadcast_to(density, (zs, points))], axis=1
-    )
-    got = lax.all_to_all(sent[:, None], Z, 0, 0, tiled=True).reshape(zs, own + 1, points)
-    rotated = got[:, :own].transpose(1, 0, 2).reshape(own, zs * points)
-    return rotated, got[:, own].reshape(zs * points)
+    largest = jnp.max(jnp.abs(new), axis=0)
+    told = jnp.concatenate([partial, largest]).reshape(1, -1)
+    heard = gathered(told, "x").reshape(xs, 2, 2, points // 2)
+    power = exponent(largest)
+    sent = (new.reshape(zs, own, points) * jnp.exp2(-power)).astype(jnp.float16)
+    sent = sent.reshape(zs, own, 2, points // 2).transpose(0, 2, 1, 3).reshape(zs, 2 * own, points // 2)
+    density = jnp.sum(heard[:, 0], axis=0) / jnp.float32(bands)
+    level = exponent(jnp.max(heard[:, 1], axis=0))
+    scaled = (density * jnp.exp2(-level)) * jnp.exp2(-level)
+    high = lax.reduce_precision(scaled, 5, 10)
+    extra = jnp.concatenate([high, (scaled - high) * 2048.0, power.reshape(2, -1), level]).astype(jnp.float16)
+    extra = jnp.broadcast_to(extra[None], (zs, *extra.shape))
+    got = lax.all_to_all(jnp.concatenate([sent, extra], 1), Z, 0, 0, tiled=True).astype(jnp.float32)
+    extra = got[:, 2 * own :].reshape(zs, 4, 2, points // 2)
+    rotated = got[:, : 2 * own].reshape(zs, 2, own, points // 2) * jnp.exp2(extra[:, 2])[:, :, None]
+    rotated = rotated.transpose(2, 0, 1, 3).reshape(own, zs * points)
+    level = jnp.exp2(extra[:, 3])
+    density = ((extra[:, 0] + extra[:, 1] * (1.0 / 2048.0)) * level) * level
+    return rotated, density.reshape(zs * points)
 
 
 def solution(mesh):

time: 140 us -> 136 us (0.971)
  blocking collectives: 104 us -> 101 us
    all_to_all x1, blocking collectives: 26.9 us -> 23.4 us  [local(): lax.all_to_all(jnp.concatenate([sent, extra], 1), Z, 0, 0, tiled=True)]
where the time goes in v2:
time: 136 us
  blocking collectives  101 us (74%)
  starting transfers between devices  14.4 us (11%)
  waiting for transfers between devices  10.7 us (8%)
  local copies, waits for them, and re-layouts  6.66 us (5%)
  other arithmetic  2.15 us (2%)
    all_to_all x1, blocking collectives, local(): lax.all_to_all(jnp.concatenate([blocks, quarters], 1), Z, 0, 0, tiled=True)  61.6 us
    all_to_all x1, blocking collectives, local(): lax.all_to_all(jnp.concatenate([sent, extra], 1), Z, 0, 0, tiled=True)  23.4 us
    all_gather x1, blocking collectives, local(): mine = lax.all_gather(met[:, own:].reshape(zs * cols * pair, run), 'zl')  15.5 us
    all_to_all x2, starting transfers between devices, gathered(): return lax.all_to_all(copies, axis, 0, 0, tiled=True)  12.4 us
    all_to_all x2, waiting for transfers between devices, gathered(): return lax.all_to_all(copies, axis, 0, 0, tiled=True)  9.7 us
  transfers between devices with their start and end apart: 3, of which 3 were waited for; matrix products, arithmetic and copies ran while one was open for 2% of the time, Pallas kernels for 0%

profile of v2, /device:TPU:80, one launch (start us, length us, event | category | flops | bytes accessed | tf_op | source)
XLA Modules:
  0.0 135.8 jit_solution(14074049480930648650)
XLA Ops:
  0.6 0.0 copy-start
  0.6 0.9 copy.69
  1.6 0.0 copy-done
  1.6 0.2 reshape.125
  1.9 0.2 reshape.126
  2.2 0.1 copy.58
  2.3 61.6 %all_to_all.20 = bf16[16,32,256]{2,1,0:T(8,128)(2,1)S(1)} all-to-all(bf16[16,32,256]{2,1,0:T(8,128)(2,1)S(1)} %copy.58), channel_id=1, replica_groups=mesh['frag'=2,'zh'=4,'zl'=4,'x'=8,'slab'=2] {'zh','zl'}, dimensions={0} | all-to-all | bytes 524288 | tf_op jit(solution)/shard_map/all_to_all | solution.py:33
  64.0 1.1 broadcast_in_dim.30
  65.0 7.3 %all-to-all-start.1 = ((bf16[8,256,256]{2,1,0:T(8,128)(2,1)}), bf16[8,256,256]{2,1,0:T(8,128)(2,1)S(1)}, u32[]{:S(2)}, u32[]{:S(2)}) async-start(bf16[8,256,256]{2,1,0:T(8,128)(2,1)} %broadcast_in_dim.30), calls=%async_computation.1 | async-start | bytes 2097152 | tf_op jit(solution)/shard_map/all_to_all | solution.py:14
  72.3 15.5 %all_gather.3 = bf16[4,256,256]{2,1,0:T(8,128)(2,1)S(1)} all-gather(bf16[1,256,256]{2,1,0:T(8,128)(2,1)S(1)} %bitcast.41), channel_id=1, replica_groups=mesh['frag'=2,'zh'=4,'zl'=4,'x'=8,'slab'=2] {'zl'}, dimensions={0}, use_global_device_ids=true | all-gather | bytes 655360 | tf_op jit(solution)/shard_map/all_gather | solution.py:35
  87.9 1.9 %collective-permute-start = (bf16[4,256,256]{2,1,0:T(8,128)(2,1)S(1)}, bf16[4,256,256]{2,1,0:T(8,128)(2,1)S(1)}, u32[]{:S(2)}, u32[]{:S(2)}) collective-permute-start(bf16[4,256,256]{2,1,0:T(8,128)(2,1)S(1)} %all_gather.3), channel_id=1, source_target_pairs={{0,1},{1,0},{2,3},{3,2},{4,5},{5,4},{6,7},{7,6},{8,9},{9,8},{10,11... | collective-permute-start | bytes 1572872 | tf_op jit(solution)/shard_map/ppermute | solution.py:36
  89.8 0.0 copy-start.1
  89.8 0.7 copy-done.1
  90.5 0.1 reshape.131
  90.7 0.1 mul.67
  90.7 1.0 collective-permute-done
  91.7 0.1 broadcast_select_fusion.1
  91.8 0.2 stack.9
  92.0 0.2 stack.10
  92.2 1.2 copy_bitcast_fusion
  93.4 0.8 reshape.128
  94.2 2.1 %all-to-all-done.1 = bf16[8,256,256]{2,1,0:T(8,128)(2,1)S(1)} async-done(((bf16[8,256,256]{2,1,0:T(8,128)(2,1)}), bf16[8,256,256]{2,1,0:T(8,128)(2,1)S(1)}, u32[]{:S(2)}, u32[]{:S(2)}) %all-to-all-start.1) | async-done | bytes 1048608 | tf_op jit(solution)/shard_map/all_to_all | solution.py:14
  96.3 0.5 fusion
  96.8 0.6 broadcast_in_dim.31
  97.4 5.1 %all-to-all-start.2 = ((f32[8,1,512]{2,1,0:T(1,128)}), f32[8,1,512]{2,1,0:T(1,128)S(1)}, u32[]{:S(2)}, u32[]{:S(2)}) async-start(f32[8,1,512]{2,1,0:T(1,128)} %broadcast_in_dim.31), calls=%async_computation.2 | async-start | bytes 32768 | tf_op jit(solution)/shard_map/all_to_all | solution.py:14
  102.6 0.1 reshape.129
  102.7 7.6 %all-to-all-done.2 = f32[8,1,512]{2,1,0:T(1,128)S(1)} async-done(((f32[8,1,512]{2,1,0:T(1,128)}), f32[8,1,512]{2,1,0:T(1,128)S(1)}, u32[]{:S(2)}, u32[]{:S(2)}) %all-to-all-start.2) | async-done | bytes 16416 | tf_op jit(solution)/shard_map/all_to_all | solution.py:14
  110.5 23.4 %all_to_all.21 = f16[16,40,128]{2,1,0:T(8,128)(2,1)S(1)} all-to-all(f16[16,40,128]{2,1,0:T(8,128)(2,1)S(1)} %pad_maximum_fusion.2), channel_id=1, replica_groups=mesh['frag'=2,'zh'=4,'zl'=4,'x'=8,'slab'=2] {'zh','zl'}, dimensions={0} | all-to-all | bytes 327680 | tf_op jit(solution)/shard_map/all_to_all | solution.py:58
  134.1 0.1 copy.65
  134.3 0.9 reshape.135
  135.2 0.6 multiply_multiply_fusion.1
  (26 shorter events, 0.5 us)
Async XLA Ops:
  0.6 0.9 copy-start
  65.0 31.3 %all-to-all-start.1 = ((bf16[8,256,256]{2,1,0:T(8,128)(2,1)}), bf16[8,256,256]{2,1,0:T(8,128)(2,1)S(1)}, u32[]{:S(2)}, u32[]{:S(2)}) async-start(bf16[8,256,256]{2,1,0:T(8,128)(2,1)} %broadcast_in_dim.30), calls=%async_computation.1 | async-start | bytes 2097152 | tf_op jit(solution)/shard_map/all_to_all | solution.py:14
  87.9 3.8 %collective-permute-start = (bf16[4,256,256]{2,1,0:T(8,128)(2,1)S(1)}, bf16[4,256,256]{2,1,0:T(8,128)(2,1)S(1)}, u32[]{:S(2)}, u32[]{:S(2)}) collective-permute-start(bf16[4,256,256]{2,1,0:T(8,128)(2,1)S(1)} %all_gather.3), channel_id=1, source_target_pairs={{0,1},{1,0},{2,3},{3,2},{4,5},{5,4},{6,7},{7,6},{8,9},{9,8},{10,11... | collective-permute-start | bytes 1572872 | tf_op jit(solution)/shard_map/ppermute | solution.py:36
  89.8 0.7 copy-start.1
  97.4 12.9 %all-to-all-start.2 = ((f32[8,1,512]{2,1,0:T(1,128)}), f32[8,1,512]{2,1,0:T(1,128)S(1)}, u32[]{:S(2)}, u32[]{:S(2)}) async-start(f32[8,1,512]{2,1,0:T(1,128)} %broadcast_in_dim.31), calls=%async_computation.2 | async-start | bytes 32768 | tf_op jit(solution)/shard_map/all_to_all | solution.py:14
